TPU v7x, 32 devices: a whole 2x2x4 slice. The times are simulated.
32 devices in a mesh: rows: 4 (over z), feat: 8 (over y, x, core).
Axes of the slice: x: 2, y: 2, z: 4, core: 2. Of those that a mesh axis runs over, the one named last changes fastest.
Arguments:
- codes: int32 [65536, 512], P(('rows', 'feat')), may hold values from 0 to 255, as said below
- node_ids: int32 [2, 65536], P(None, ('rows', 'feat')), may hold values from 0 to 3
- bag_counts: int32 [2, 65536], P(None, ('rows', 'feat')), may hold values from 0 to 3
- labels: int32 [65536], P(('rows', 'feat')), may hold values from 0 to 1
Outputs:
- feature_gain: float32 [2, 4, 512], P(None, None, 'feat')
- node_gain: float32 [2, 4], replicated
Inputs may be any that keep to these rules, and one draw needn't show every extreme that they name: Each feature's codes lie below a cap of that feature; bins above the cap are empty.
All inputs are finite; a program needn't handle non-finite values.
Results may differ from a plain program's by a relative error of at most 0.0003.
Values sent between devices are 32-bit elements; how exact they have to be, the bound alone decides.
A program may use at most 64 MiB of HBM per device.

v0:
```python
import math
import jax
import jax.numpy as jnp
from jax import lax
from jax.sharding import PartitionSpec as P

BINS = 256
CLASSES = 2
TREES = 2
NODES = 4


def make_weights(node_ids, bag_counts, labels):
    trees, count_rows = node_ids.shape
    node_range = jnp.arange(NODES, dtype=jnp.int32)
    class_range = jnp.arange(CLASSES, dtype=jnp.int32)
    node_hit = (node_ids[:, :, None] == node_range).astype(jnp.float32)
    class_hit = (labels[:, None] == class_range).astype(jnp.float32)
    weights = (
        bag_counts.astype(jnp.float32)[:, :, None, None]
        * node_hit[:, :, :, None]
        * class_hit[None, :, None, :]
    )
    return (
        jnp.transpose(weights, (1, 0, 2, 3))
        .reshape(count_rows, trees * NODES * CLASSES)
        .astype(jnp.bfloat16)
    )


def split_gains(left):
    feats = left.shape[0]
    left = left.reshape(feats, TREES, NODES, CLASSES, left.shape[-1])
    total = left[..., -1:]
    n_left = jnp.sum(left, axis=3, keepdims=True)
    n_total = jnp.sum(total, axis=3, keepdims=True)
    n_right = n_total - n_left
    frac = n_left / jnp.maximum(n_total, 1.0)
    spread_terms = (left - total * frac) ** 2
    scaled = n_total / (jnp.maximum(n_left, 1.0) * jnp.maximum(n_right, 1.0))
    spread = jnp.sum(spread_terms * scaled, axis=3)
    best = jnp.max(spread, axis=-1)
    return jnp.transpose(best, (1, 2, 0))


def gains_of(hist):
    bin_index = jnp.arange(BINS, dtype=jnp.int32)
    upper = (bin_index[:, None] <= bin_index[None, :]).astype(jnp.float32)
    left = jnp.einsum("fsb,bk->fsk", hist, upper, precision=lax.Precision.HIGHEST)
    return split_gains(left)


def histogram_of(columns, weights):
    count_rows, count = columns.shape
    block_size = math.gcd(count, 32)
    blocks = jnp.transpose(columns.reshape(count_rows, count // block_size, block_size), (1, 0, 2))
    bin_index = jnp.arange(BINS, dtype=jnp.int32)

    def one_block(column_block):
        onehot = (column_block[:, :, None] == bin_index).astype(jnp.bfloat16)
        return jnp.einsum("rfb,rs->fsb", onehot, weights, preferred_element_type=jnp.float32)

    summed = lax.map(one_block, blocks)
    return summed.reshape(count, weights.shape[1], BINS)


def on_device(codes, node_ids, bag_counts, labels):
    weights = make_weights(node_ids, bag_counts, labels)
    partial_hist = lax.psum_scatter(
        histogram_of(codes, weights), "feat", scatter_dimension=0, tiled=True
    )
    hist = lax.psum(partial_hist, "rows")
    feature_gain = gains_of(hist)
    node_gain = lax.pmax(jnp.max(feature_gain, axis=2), "feat")
    return (feature_gain, node_gain)


def solution(mesh):
    return jax.shard_map(
        on_device,
        mesh=mesh,
        in_specs=(
            P(("rows", "feat"), None),
            P(None, ("rows", "feat")),
            P(None, ("rows", "feat")),
            P(("rows", "feat")),
        ),
        out_specs=(P(None, None, "feat"), P()),
        check_vma=False,
    )
```

profile of v0, /device:TPU:0, one launch (start us, length us, event | category | flops | bytes accessed | tf_op | source)
XLA Modules:
  0.0 460.7 jit_solution(4944158148707824612)
XLA Ops:
  7.2 5.4 %copy.20 = s32[2048,512]{0,1:T(8,128)} copy(s32[2048,512]{1,0:T(8,128)} %param.6) | data formatting | bytes 8388608 | tf_op args[0]
  12.8 286.6 %while.11 = (s32[]{:T(128)}, f32[16,32,16,256]{3,2,1,0:T(8,128)}, s32[16,2048,32]{1,2,0:T(8,128)}, f32[2048,2]{0,1:T(2,128)S(1)}, f32[2048,2,4]{0,2,1:T(4,128)S(1)}, /*index=5*/s32[]{:T(128)}) while((s32[]{:T(128)}, f32[16,32,16,256]{3,2,1,0:T(8,128)}, s32[16,2048,32]{1,2,0:T(8,128)}, f32[2048,2]{0,1:T(2,128)S(1)}, ...), condition=%wide.region_1.2_spmd.clone, body=%wide.region_0.1_spmd.clone.sunk | while | flops 553713664 | bytes 1655369 | solution.py:63
  12.8 1.0 dynamic-slice_bitcast_fusion.2
  13.8 0.1 multiply_convert_fusion.2
  13.9 16.8 %fusion.19 = f32[16,32,16,256]{3,2,1,0:T(8,128)} fusion(f32[16,32,16,256]{3,2,1,0:T(8,128)} %get-tuple-element.97, s32[]{:T(128)} %get-tuple-element.96, bf16[2048,16,1]{0,1,2:T(8,128)(2,1)S(1)} %reshape.85, s32[2048,32]{0,1:T(8,128)S(1)} %dynamic-slice_bitcast_fusion.2), kind=kOutput, calls=%fused_computation.6.clone.2 | convolution fusion | flops 553648128 | bytes 852480 | tf_op jit(solution)/shard_map/while/body/eval_jaxpr/rfb,rs->fsb/dot_general | solution.py:61
  30.7 1.0 dynamic-slice_bitcast_fusion.2
  31.7 0.1 multiply_convert_fusion.2
  31.8 16.8 %fusion.19 = f32[16,32,16,256]{3,2,1,0:T(8,128)} fusion(f32[16,32,16,256]{3,2,1,0:T(8,128)} %get-tuple-element.97, s32[]{:T(128)} %get-tuple-element.96, bf16[2048,16,1]{0,1,2:T(8,128)(2,1)S(1)} %reshape.85, s32[2048,32]{0,1:T(8,128)S(1)} %dynamic-slice_bitcast_fusion.2), kind=kOutput, calls=%fused_computation.6.clone.2 | convolution fusion | flops 553648128 | bytes 852480 | tf_op jit(solution)/shard_map/while/body/eval_jaxpr/rfb,rs->fsb/dot_general | solution.py:61
  48.6 1.0 dynamic-slice_bitcast_fusion.2
  49.6 0.1 multiply_convert_fusion.2
  49.7 16.8 %fusion.19 = f32[16,32,16,256]{3,2,1,0:T(8,128)} fusion(f32[16,32,16,256]{3,2,1,0:T(8,128)} %get-tuple-element.97, s32[]{:T(128)} %get-tuple-element.96, bf16[2048,16,1]{0,1,2:T(8,128)(2,1)S(1)} %reshape.85, s32[2048,32]{0,1:T(8,128)S(1)} %dynamic-slice_bitcast_fusion.2), kind=kOutput, calls=%fused_computation.6.clone.2 | convolution fusion | flops 553648128 | bytes 852480 | tf_op jit(solution)/shard_map/while/body/eval_jaxpr/rfb,rs->fsb/dot_general | solution.py:61
  66.5 1.0 dynamic-slice_bitcast_fusion.2
  67.5 0.1 multiply_convert_fusion.2
  67.6 16.8 %fusion.19 = f32[16,32,16,256]{3,2,1,0:T(8,128)} fusion(f32[16,32,16,256]{3,2,1,0:T(8,128)} %get-tuple-element.97, s32[]{:T(128)} %get-tuple-element.96, bf16[2048,16,1]{0,1,2:T(8,128)(2,1)S(1)} %reshape.85, s32[2048,32]{0,1:T(8,128)S(1)} %dynamic-slice_bitcast_fusion.2), kind=kOutput, calls=%fused_computation.6.clone.2 | convolution fusion | flops 553648128 | bytes 852480 | tf_op jit(solution)/shard_map/while/body/eval_jaxpr/rfb,rs->fsb/dot_general | solution.py:61
  84.4 1.0 dynamic-slice_bitcast_fusion.2
  85.4 0.1 multiply_convert_fusion.2
  85.5 16.8 %fusion.19 = f32[16,32,16,256]{3,2,1,0:T(8,128)} fusion(f32[16,32,16,256]{3,2,1,0:T(8,128)} %get-tuple-element.97, s32[]{:T(128)} %get-tuple-element.96, bf16[2048,16,1]{0,1,2:T(8,128)(2,1)S(1)} %reshape.85, s32[2048,32]{0,1:T(8,128)S(1)} %dynamic-slice_bitcast_fusion.2), kind=kOutput, calls=%fused_computation.6.clone.2 | convolution fusion | flops 553648128 | bytes 852480 | tf_op jit(solution)/shard_map/while/body/eval_jaxpr/rfb,rs->fsb/dot_general | solution.py:61
  102.3 1.0 dynamic-slice_bitcast_fusion.2
  103.3 0.1 multiply_convert_fusion.2
  103.4 16.8 %fusion.19 = f32[16,32,16,256]{3,2,1,0:T(8,128)} fusion(f32[16,32,16,256]{3,2,1,0:T(8,128)} %get-tuple-element.97, s32[]{:T(128)} %get-tuple-element.96, bf16[2048,16,1]{0,1,2:T(8,128)(2,1)S(1)} %reshape.85, s32[2048,32]{0,1:T(8,128)S(1)} %dynamic-slice_bitcast_fusion.2), kind=kOutput, calls=%fused_computation.6.clone.2 | convolution fusion | flops 553648128 | bytes 852480 | tf_op jit(solution)/shard_map/while/body/eval_jaxpr/rfb,rs->fsb/dot_general | solution.py:61
  120.2 1.0 dynamic-slice_bitcast_fusion.2
  121.2 0.1 multiply_convert_fusion.2
  121.3 16.8 %fusion.19 = f32[16,32,16,256]{3,2,1,0:T(8,128)} fusion(f32[16,32,16,256]{3,2,1,0:T(8,128)} %get-tuple-element.97, s32[]{:T(128)} %get-tuple-element.96, bf16[2048,16,1]{0,1,2:T(8,128)(2,1)S(1)} %reshape.85, s32[2048,32]{0,1:T(8,128)S(1)} %dynamic-slice_bitcast_fusion.2), kind=kOutput, calls=%fused_computation.6.clone.2 | convolution fusion | flops 553648128 | bytes 852480 | tf_op jit(solution)/shard_map/while/body/eval_jaxpr/rfb,rs->fsb/dot_general | solution.py:61
  138.1 1.0 dynamic-slice_bitcast_fusion.2
  139.1 0.1 multiply_convert_fusion.2
  139.2 16.8 %fusion.19 = f32[16,32,16,256]{3,2,1,0:T(8,128)} fusion(f32[16,32,16,256]{3,2,1,0:T(8,128)} %get-tuple-element.97, s32[]{:T(128)} %get-tuple-element.96, bf16[2048,16,1]{0,1,2:T(8,128)(2,1)S(1)} %reshape.85, s32[2048,32]{0,1:T(8,128)S(1)} %dynamic-slice_bitcast_fusion.2), kind=kOutput, calls=%fused_computation.6.clone.2 | convolution fusion | flops 553648128 | bytes 852480 | tf_op jit(solution)/shard_map/while/body/eval_jaxpr/rfb,rs->fsb/dot_general | solution.py:61
  156.1 1.0 dynamic-slice_bitcast_fusion.2
  157.0 0.1 multiply_convert_fusion.2
  157.1 16.8 %fusion.19 = f32[16,32,16,256]{3,2,1,0:T(8,128)} fusion(f32[16,32,16,256]{3,2,1,0:T(8,128)} %get-tuple-element.97, s32[]{:T(128)} %get-tuple-element.96, bf16[2048,16,1]{0,1,2:T(8,128)(2,1)S(1)} %reshape.85, s32[2048,32]{0,1:T(8,128)S(1)} %dynamic-slice_bitcast_fusion.2), kind=kOutput, calls=%fused_computation.6.clone.2 | convolution fusion | flops 553648128 | bytes 852480 | tf_op jit(solution)/shard_map/while/body/eval_jaxpr/rfb,rs->fsb/dot_general | solution.py:61
  174.0 1.0 dynamic-slice_bitcast_fusion.2
  174.9 0.1 multiply_convert_fusion.2
  175.0 16.8 %fusion.19 = f32[16,32,16,256]{3,2,1,0:T(8,128)} fusion(f32[16,32,16,256]{3,2,1,0:T(8,128)} %get-tuple-element.97, s32[]{:T(128)} %get-tuple-element.96, bf16[2048,16,1]{0,1,2:T(8,128)(2,1)S(1)} %reshape.85, s32[2048,32]{0,1:T(8,128)S(1)} %dynamic-slice_bitcast_fusion.2), kind=kOutput, calls=%fused_computation.6.clone.2 | convolution fusion | flops 553648128 | bytes 852480 | tf_op jit(solution)/shard_map/while/body/eval_jaxpr/rfb,rs->fsb/dot_general | solution.py:61
  191.9 1.0 dynamic-slice_bitcast_fusion.2
  192.8 0.1 multiply_convert_fusion.2
  192.9 16.8 %fusion.19 = f32[16,32,16,256]{3,2,1,0:T(8,128)} fusion(f32[16,32,16,256]{3,2,1,0:T(8,128)} %get-tuple-element.97, s32[]{:T(128)} %get-tuple-element.96, bf16[2048,16,1]{0,1,2:T(8,128)(2,1)S(1)} %reshape.85, s32[2048,32]{0,1:T(8,128)S(1)} %dynamic-slice_bitcast_fusion.2), kind=kOutput, calls=%fused_computation.6.clone.2 | convolution fusion | flops 553648128 | bytes 852480 | tf_op jit(solution)/shard_map/while/body/eval_jaxpr/rfb,rs->fsb/dot_general | solution.py:61
  209.8 1.0 dynamic-slice_bitcast_fusion.2
  210.8 0.1 multiply_convert_fusion.2
  210.8 16.8 %fusion.19 = f32[16,32,16,256]{3,2,1,0:T(8,128)} fusion(f32[16,32,16,256]{3,2,1,0:T(8,128)} %get-tuple-element.97, s32[]{:T(128)} %get-tuple-element.96, bf16[2048,16,1]{0,1,2:T(8,128)(2,1)S(1)} %reshape.85, s32[2048,32]{0,1:T(8,128)S(1)} %dynamic-slice_bitcast_fusion.2), kind=kOutput, calls=%fused_computation.6.clone.2 | convolution fusion | flops 553648128 | bytes 852480 | tf_op jit(solution)/shard_map/while/body/eval_jaxpr/rfb,rs->fsb/dot_general | solution.py:61
  227.7 1.0 dynamic-slice_bitcast_fusion.2
  228.7 0.1 multiply_convert_fusion.2
  228.8 16.8 %fusion.19 = f32[16,32,16,256]{3,2,1,0:T(8,128)} fusion(f32[16,32,16,256]{3,2,1,0:T(8,128)} %get-tuple-element.97, s32[]{:T(128)} %get-tuple-element.96, bf16[2048,16,1]{0,1,2:T(8,128)(2,1)S(1)} %reshape.85, s32[2048,32]{0,1:T(8,128)S(1)} %dynamic-slice_bitcast_fusion.2), kind=kOutput, calls=%fused_computation.6.clone.2 | convolution fusion | flops 553648128 | bytes 852480 | tf_op jit(solution)/shard_map/while/body/eval_jaxpr/rfb,rs->fsb/dot_general | solution.py:61
  245.6 1.0 dynamic-slice_bitcast_fusion.2
  246.6 0.1 multiply_convert_fusion.2
  246.7 16.8 %fusion.19 = f32[16,32,16,256]{3,2,1,0:T(8,128)} fusion(f32[16,32,16,256]{3,2,1,0:T(8,128)} %get-tuple-element.97, s32[]{:T(128)} %get-tuple-element.96, bf16[2048,16,1]{0,1,2:T(8,128)(2,1)S(1)} %reshape.85, s32[2048,32]{0,1:T(8,128)S(1)} %dynamic-slice_bitcast_fusion.2), kind=kOutput, calls=%fused_computation.6.clone.2 | convolution fusion | flops 553648128 | bytes 852480 | tf_op jit(solution)/shard_map/while/body/eval_jaxpr/rfb,rs->fsb/dot_general | solution.py:61
  263.5 1.0 dynamic-slice_bitcast_fusion.2
  264.6 16.8 %fusion.19 = f32[16,32,16,256]{3,2,1,0:T(8,128)} fusion(f32[16,32,16,256]{3,2,1,0:T(8,128)} %get-tuple-element.97, s32[]{:T(128)} %get-tuple-element.96, bf16[2048,16,1]{0,1,2:T(8,128)(2,1)S(1)} %reshape.85, s32[2048,32]{0,1:T(8,128)S(1)} %dynamic-slice_bitcast_fusion.2), kind=kOutput, calls=%fused_computation.6.clone.2 | convolution fusion | flops 553648128 | bytes 852480 | tf_op jit(solution)/shard_map/while/body/eval_jaxpr/rfb,rs->fsb/dot_general | solution.py:61
  281.4 1.0 dynamic-slice_bitcast_fusion.2
  282.4 0.1 multiply_convert_fusion.2
  282.5 16.8 %fusion.19 = f32[16,32,16,256]{3,2,1,0:T(8,128)} fusion(f32[16,32,16,256]{3,2,1,0:T(8,128)} %get-tuple-element.97, s32[]{:T(128)} %get-tuple-element.96, bf16[2048,16,1]{0,1,2:T(8,128)(2,1)S(1)} %reshape.85, s32[2048,32]{0,1:T(8,128)S(1)} %dynamic-slice_bitcast_fusion.2), kind=kOutput, calls=%fused_computation.6.clone.2 | convolution fusion | flops 553648128 | bytes 852480 | tf_op jit(solution)/shard_map/while/body/eval_jaxpr/rfb,rs->fsb/dot_general | solution.py:61
  299.4 74.3 %reduce-scatter.2.cloned.1.call-done = f32[64,16,256]{2,1,0:T(8,128)} async-done(((f32[512,16,256]{2,1,0:T(8,128)}), f32[64,16,256]{2,1,0:T(8,128)}) %reduce-scatter.2.cloned.1.call-update) | async-done | bytes 1048592 | tf_op jit(solution)/shard_map/reduce_scatter | solution.py:69
  373.8 54.3 %all-reduce.2.cloned.1.call-done = f32[64,16,256]{2,1,0:T(8,128)} async-done(((f32[64,16,256]{2,1,0:T(8,128)}), f32[64,16,256]{2,1,0:T(8,128)}) %all-reduce.2.cloned.1.call-update) | async-done | bytes 1048592 | tf_op jit(solution)/shard_map/psum | solution.py:72
  428.0 1.8 fusion.9
  429.9 0.6 reshape.80
  430.5 1.4 fusion.12
  431.9 0.1 copy.29
  432.0 0.1 copy.23
  432.1 1.5 reduce_sum.27
  433.6 3.1 copy.28
  436.8 0.4 broadcast_divide_fusion
  437.1 2.0 multiply_reduce_fusion
  439.1 0.3 reduce_max.18
  439.4 0.1 copy.26
  439.5 0.1 bitcast_reduce_fusion
  439.6 14.3 %pmax.7 = f32[2,4]{1,0:T(2,128)} all-reduce(f32[2,4]{1,0:T(2,128)S(1)} %bitcast_reduce_fusion), channel_id=1, replica_groups=mesh['rows'=4,'feat'=8] {'feat'}, use_global_device_ids=true, to_apply=%region_9.10 | all-reduce | flops 8 | bytes 64 | tf_op jit(solution)/shard_map/pmax | solution.py:74
  (34 shorter events, 0.7 us)
Async XLA Ops:
  7.2 5.5 %copy-start.1 = (s32[2,2048]{1,0:T(2,128)S(1)}, s32[2,2048]{1,0:T(2,128)}, u32[]{:S(2)}) copy-start(s32[2,2048]{1,0:T(2,128)} %param.8) | copy-start | bytes 49156
  7.2 5.5 %copy-start.3 = (s32[2048]{0:T(1024)S(1)}, s32[2048]{0:T(1024)}, u32[]{:S(2)}) copy-start(s32[2048]{0:T(1024)} %param.9) | copy-start | bytes 24580
  7.2 5.5 %copy-start.2 = (s32[2,2048]{1,0:T(2,128)S(1)}, s32[2,2048]{1,0:T(2,128)}, u32[]{:S(2)}) copy-start(s32[2,2048]{1,0:T(2,128)} %param.7) | copy-start | bytes 49156
  7.2 366.5 %reduce-scatter.2.cloned.1.call-start = ((), (), s32[]{:S(2)}) async-start(), calls=%async_computation.1 | async-start | bytes 9437184 | tf_op jit(solution)/shard_map/reduce_scatter | solution.py:69
  299.4 128.7 %all-reduce.2.cloned.1.call-start = ((), (), s32[]{:S(2)}) async-start(), calls=%async_computation.2 | async-start | bytes 2097152 | tf_op jit(solution)/shard_map/psum | solution.py:72
  439.5 14.3 %copy-start = (f32[64,2,4]{0,2,1:T(4,128)}, f32[64,2,4]{0,2,1:T(4,128)S(1)}, u32[]{:S(2)}) copy-start(f32[64,2,4]{0,2,1:T(4,128)S(1)} %copy.26) | copy-start | bytes 6148
Sparse Core Ops, SparseCore 0:
  299.5 74.2 reduce-scatter.1
  376.1 51.8 all-reduce.1
where the time goes:
time: 461 us
  matrix products  271 us (59%)
  waiting for transfers between devices  129 us (28%)
  local copies, waits for them, and re-layouts  25.5 us (6%)
  blocking collectives  14.3 us (3%)
  between operations  14.2 us (3%)
  other arithmetic  6.47 us (1%)
    dot_general x16, matrix products, one_block(): jnp.einsum('rfb,rs->fsb', onehot, weights, preferred_element_type=jnp.flo...  269 us
    reduce_scatter x1, waiting for transfers between devices, on_device(): lax.psum_scatter(histogram_of(codes, weights), 'feat', scatter_dimension=...  74.3 us
    psum x1, waiting for transfers between devices, on_device(): hist = lax.psum(partial_hist, 'rows')  54.3 us
    eq x16, local copies, waits for them, and re-layouts, one_block(): onehot = (column_block[:, :, None] == bin_index).astype(jnp.bfloat16)  15.5 us
    pmax x1, blocking collectives, on_device(): node_gain = lax.pmax(jnp.max(feature_gain, axis=2), 'feat')  14.3 us
  transfers between devices with their start and end apart: 2, of which 2 were waited for; matrix products, arithmetic and copies ran while one was open for 0% of the time, Pallas kernels for 0%

commit v1 on v0

--- a/solution.py
+++ b/solution.py
@@ -69,7 +69,9 @@
     partial_hist = lax.psum_scatter(
         histogram_of(codes, weights), "feat", scatter_dimension=0, tiled=True
     )
-    hist = lax.psum(partial_hist, "rows")
+    hist = partial_hist
+    for hop in (1, 2):
+        hist = hist + lax.ppermute(hist, "rows", [(dev, dev ^ hop) for dev in range(4)])
     feature_gain = gains_of(hist)
     node_gain = lax.pmax(jnp.max(feature_gain, axis=2), "feat")
     return (feature_gain, node_gain)

time: 461 us -> 478 us (1.037)
  waiting for transfers between devices: 129 us -> 143 us
    ppermute x0 -> x2, waiting for transfers between devices: none -> 68.2 us  [on_device(): lax.ppermute(hist, 'rows', [(dev, dev ^ hop) for dev in range(4)])]
    psum x1 -> x0, waiting for transfers between devices: 54.3 us -> none  [on_device(): hist = lax.psum(partial_hist, 'rows')]
  transfers between devices with their start and end apart: 2 -> 3, of which waited for: 2 -> 3; matrix products, arithmetic and copies ran while one was open for 0% -> 0% of each run, Pallas kernels for 0% -> 0%
where the time goes in v1:
time: 478 us; the launch traced here: 477 us
  matrix products  270 us (56%)
  waiting for transfers between devices  143 us (30%)
  local copies, waits for them, and re-layouts  25.5 us (5%)
  between operations  14.2 us (3%)
  blocking collectives  12.5 us (3%)
  other arithmetic  7.91 us (2%)
    dot_general x16, matrix products, one_block(): jnp.einsum('rfb,rs->fsb', onehot, weights, preferred_element_type=jnp.flo...  269 us
    reduce_scatter x1, waiting for transfers between devices, on_device(): lax.psum_scatter(histogram_of(codes, weights), 'feat', scatter_dimension=...  74.4 us
    ppermute x2, waiting for transfers between devices, on_device(): lax.ppermute(hist, 'rows', [(dev, dev ^ hop) for dev in range(4)])  68.2 us
    eq x16, local copies, waits for them, and re-layouts, one_block(): onehot = (column_block[:, :, None] == bin_index).astype(jnp.bfloat16)  15.5 us
    pmax x1, blocking collectives, on_device(): node_gain = lax.pmax(jnp.max(feature_gain, axis=2), 'feat')  12.5 us
  transfers between devices with their start and end apart: 3, of which 3 were waited for; matrix products, arithmetic and copies ran while one was open for 0% of the time, Pallas kernels for 0%

profile of v1, /device:TPU:0, one launch (start us, length us, event | category | flops | bytes accessed | tf_op | source)
XLA Modules:
  0.0 477.2 jit_solution(11053537814950222885)
XLA Ops:
  7.2 5.4 %copy.20 = s32[2048,512]{0,1:T(8,128)} copy(s32[2048,512]{1,0:T(8,128)} %param.6) | data formatting | bytes 8388608 | tf_op args[0]
  12.8 286.6 %while.11 = (s32[]{:T(128)}, f32[16,32,16,256]{3,2,1,0:T(8,128)}, s32[16,2048,32]{1,2,0:T(8,128)}, f32[2048,2]{0,1:T(2,128)S(1)}, f32[2048,2,4]{0,2,1:T(4,128)S(1)}, /*index=5*/s32[]{:T(128)}) while((s32[]{:T(128)}, f32[16,32,16,256]{3,2,1,0:T(8,128)}, s32[16,2048,32]{1,2,0:T(8,128)}, f32[2048,2]{0,1:T(2,128)S(1)}, ...), condition=%wide.region_1.2_spmd.clone, body=%wide.region_0.1_spmd.clone.sunk | while | flops 553713664 | bytes 1655369 | solution.py:63
  12.8 1.0 dynamic-slice_bitcast_fusion.2
  13.9 16.8 %fusion.19 = f32[16,32,16,256]{3,2,1,0:T(8,128)} fusion(f32[16,32,16,256]{3,2,1,0:T(8,128)} %get-tuple-element.97, s32[]{:T(128)} %get-tuple-element.96, bf16[2048,16,1]{0,1,2:T(8,128)(2,1)S(1)} %reshape.85, s32[2048,32]{0,1:T(8,128)S(1)} %dynamic-slice_bitcast_fusion.2), kind=kOutput, calls=%fused_computation.6.clone.2 | convolution fusion | flops 553648128 | bytes 852480 | tf_op jit(solution)/shard_map/while/body/eval_jaxpr/rfb,rs->fsb/dot_general | solution.py:61
  30.7 1.0 dynamic-slice_bitcast_fusion.2
  31.7 0.1 multiply_convert_fusion.2
  31.8 16.8 %fusion.19 = f32[16,32,16,256]{3,2,1,0:T(8,128)} fusion(f32[16,32,16,256]{3,2,1,0:T(8,128)} %get-tuple-element.97, s32[]{:T(128)} %get-tuple-element.96, bf16[2048,16,1]{0,1,2:T(8,128)(2,1)S(1)} %reshape.85, s32[2048,32]{0,1:T(8,128)S(1)} %dynamic-slice_bitcast_fusion.2), kind=kOutput, calls=%fused_computation.6.clone.2 | convolution fusion | flops 553648128 | bytes 852480 | tf_op jit(solution)/shard_map/while/body/eval_jaxpr/rfb,rs->fsb/dot_general | solution.py:61
  48.6 1.0 dynamic-slice_bitcast_fusion.2
  49.7 16.8 %fusion.19 = f32[16,32,16,256]{3,2,1,0:T(8,128)} fusion(f32[16,32,16,256]{3,2,1,0:T(8,128)} %get-tuple-element.97, s32[]{:T(128)} %get-tuple-element.96, bf16[2048,16,1]{0,1,2:T(8,128)(2,1)S(1)} %reshape.85, s32[2048,32]{0,1:T(8,128)S(1)} %dynamic-slice_bitcast_fusion.2), kind=kOutput, calls=%fused_computation.6.clone.2 | convolution fusion | flops 553648128 | bytes 852480 | tf_op jit(solution)/shard_map/while/body/eval_jaxpr/rfb,rs->fsb/dot_general | solution.py:61
  66.5 1.0 dynamic-slice_bitcast_fusion.2
  67.6 16.8 %fusion.19 = f32[16,32,16,256]{3,2,1,0:T(8,128)} fusion(f32[16,32,16,256]{3,2,1,0:T(8,128)} %get-tuple-element.97, s32[]{:T(128)} %get-tuple-element.96, bf16[2048,16,1]{0,1,2:T(8,128)(2,1)S(1)} %reshape.85, s32[2048,32]{0,1:T(8,128)S(1)} %dynamic-slice_bitcast_fusion.2), kind=kOutput, calls=%fused_computation.6.clone.2 | convolution fusion | flops 553648128 | bytes 852480 | tf_op jit(solution)/shard_map/while/body/eval_jaxpr/rfb,rs->fsb/dot_general | solution.py:61
  84.4 1.0 dynamic-slice_bitcast_fusion.2
  85.4 0.1 multiply_convert_fusion.2
  85.5 16.8 %fusion.19 = f32[16,32,16,256]{3,2,1,0:T(8,128)} fusion(f32[16,32,16,256]{3,2,1,0:T(8,128)} %get-tuple-element.97, s32[]{:T(128)} %get-tuple-element.96, bf16[2048,16,1]{0,1,2:T(8,128)(2,1)S(1)} %reshape.85, s32[2048,32]{0,1:T(8,128)S(1)} %dynamic-slice_bitcast_fusion.2), kind=kOutput, calls=%fused_computation.6.clone.2 | convolution fusion | flops 553648128 | bytes 852480 | tf_op jit(solution)/shard_map/while/body/eval_jaxpr/rfb,rs->fsb/dot_general | solution.py:61
  102.3 1.0 dynamic-slice_bitcast_fusion.2
  103.3 0.1 multiply_convert_fusion.2
  103.4 16.8 %fusion.19 = f32[16,32,16,256]{3,2,1,0:T(8,128)} fusion(f32[16,32,16,256]{3,2,1,0:T(8,128)} %get-tuple-element.97, s32[]{:T(128)} %get-tuple-element.96, bf16[2048,16,1]{0,1,2:T(8,128)(2,1)S(1)} %reshape.85, s32[2048,32]{0,1:T(8,128)S(1)} %dynamic-slice_bitcast_fusion.2), kind=kOutput, calls=%fused_computation.6.clone.2 | convolution fusion | flops 553648128 | bytes 852480 | tf_op jit(solution)/shard_map/while/body/eval_jaxpr/rfb,rs->fsb/dot_general | solution.py:61
  120.2 1.0 dynamic-slice_bitcast_fusion.2
  121.2 0.1 multiply_convert_fusion.2
  121.3 16.8 %fusion.19 = f32[16,32,16,256]{3,2,1,0:T(8,128)} fusion(f32[16,32,16,256]{3,2,1,0:T(8,128)} %get-tuple-element.97, s32[]{:T(128)} %get-tuple-element.96, bf16[2048,16,1]{0,1,2:T(8,128)(2,1)S(1)} %reshape.85, s32[2048,32]{0,1:T(8,128)S(1)} %dynamic-slice_bitcast_fusion.2), kind=kOutput, calls=%fused_computation.6.clone.2 | convolution fusion | flops 553648128 | bytes 852480 | tf_op jit(solution)/shard_map/while/body/eval_jaxpr/rfb,rs->fsb/dot_general | solution.py:61
  138.1 1.0 dynamic-slice_bitcast_fusion.2
  139.1 0.1 multiply_convert_fusion.2
  139.2 16.8 %fusion.19 = f32[16,32,16,256]{3,2,1,0:T(8,128)} fusion(f32[16,32,16,256]{3,2,1,0:T(8,128)} %get-tuple-element.97, s32[]{:T(128)} %get-tuple-element.96, bf16[2048,16,1]{0,1,2:T(8,128)(2,1)S(1)} %reshape.85, s32[2048,32]{0,1:T(8,128)S(1)} %dynamic-slice_bitcast_fusion.2), kind=kOutput, calls=%fused_computation.6.clone.2 | convolution fusion | flops 553648128 | bytes 852480 | tf_op jit(solution)/shard_map/while/body/eval_jaxpr/rfb,rs->fsb/dot_general | solution.py:61
  156.1 1.0 dynamic-slice_bitcast_fusion.2
  157.0 0.1 multiply_convert_fusion.2
  157.1 16.8 %fusion.19 = f32[16,32,16,256]{3,2,1,0:T(8,128)} fusion(f32[16,32,16,256]{3,2,1,0:T(8,128)} %get-tuple-element.97, s32[]{:T(128)} %get-tuple-element.96, bf16[2048,16,1]{0,1,2:T(8,128)(2,1)S(1)} %reshape.85, s32[2048,32]{0,1:T(8,128)S(1)} %dynamic-slice_bitcast_fusion.2), kind=kOutput, calls=%fused_computation.6.clone.2 | convolution fusion | flops 553648128 | bytes 852480 | tf_op jit(solution)/shard_map/while/body/eval_jaxpr/rfb,rs->fsb/dot_general | solution.py:61
  174.0 1.0 dynamic-slice_bitcast_fusion.2
  174.9 0.1 multiply_convert_fusion.2
  175.0 16.8 %fusion.19 = f32[16,32,16,256]{3,2,1,0:T(8,128)} fusion(f32[16,32,16,256]{3,2,1,0:T(8,128)} %get-tuple-element.97, s32[]{:T(128)} %get-tuple-element.96, bf16[2048,16,1]{0,1,2:T(8,128)(2,1)S(1)} %reshape.85, s32[2048,32]{0,1:T(8,128)S(1)} %dynamic-slice_bitcast_fusion.2), kind=kOutput, calls=%fused_computation.6.clone.2 | convolution fusion | flops 553648128 | bytes 852480 | tf_op jit(solution)/shard_map/while/body/eval_jaxpr/rfb,rs->fsb/dot_general | solution.py:61
  191.9 1.0 dynamic-slice_bitcast_fusion.2
  192.8 0.1 multiply_convert_fusion.2
  192.9 16.8 %fusion.19 = f32[16,32,16,256]{3,2,1,0:T(8,128)} fusion(f32[16,32,16,256]{3,2,1,0:T(8,128)} %get-tuple-element.97, s32[]{:T(128)} %get-tuple-element.96, bf16[2048,16,1]{0,1,2:T(8,128)(2,1)S(1)} %reshape.85, s32[2048,32]{0,1:T(8,128)S(1)} %dynamic-slice_bitcast_fusion.2), kind=kOutput, calls=%fused_computation.6.clone.2 | convolution fusion | flops 553648128 | bytes 852480 | tf_op jit(solution)/shard_map/while/body/eval_jaxpr/rfb,rs->fsb/dot_general | solution.py:61
  209.8 1.0 dynamic-slice_bitcast_fusion.2
  210.8 0.1 multiply_convert_fusion.2
  210.8 16.8 %fusion.19 = f32[16,32,16,256]{3,2,1,0:T(8,128)} fusion(f32[16,32,16,256]{3,2,1,0:T(8,128)} %get-tuple-element.97, s32[]{:T(128)} %get-tuple-element.96, bf16[2048,16,1]{0,1,2:T(8,128)(2,1)S(1)} %reshape.85, s32[2048,32]{0,1:T(8,128)S(1)} %dynamic-slice_bitcast_fusion.2), kind=kOutput, calls=%fused_computation.6.clone.2 | convolution fusion | flops 553648128 | bytes 852480 | tf_op jit(solution)/shard_map/while/body/eval_jaxpr/rfb,rs->fsb/dot_general | solution.py:61
  227.7 1.0 dynamic-slice_bitcast_fusion.2
  228.7 0.1 multiply_convert_fusion.2
  228.8 16.8 %fusion.19 = f32[16,32,16,256]{3,2,1,0:T(8,128)} fusion(f32[16,32,16,256]{3,2,1,0:T(8,128)} %get-tuple-element.97, s32[]{:T(128)} %get-tuple-element.96, bf16[2048,16,1]{0,1,2:T(8,128)(2,1)S(1)} %reshape.85, s32[2048,32]{0,1:T(8,128)S(1)} %dynamic-slice_bitcast_fusion.2), kind=kOutput, calls=%fused_computation.6.clone.2 | convolution fusion | flops 553648128 | bytes 852480 | tf_op jit(solution)/shard_map/while/body/eval_jaxpr/rfb,rs->fsb/dot_general | solution.py:61
  245.6 1.0 dynamic-slice_bitcast_fusion.2
  246.7 16.8 %fusion.19 = f32[16,32,16,256]{3,2,1,0:T(8,128)} fusion(f32[16,32,16,256]{3,2,1,0:T(8,128)} %get-tuple-element.97, s32[]{:T(128)} %get-tuple-element.96, bf16[2048,16,1]{0,1,2:T(8,128)(2,1)S(1)} %reshape.85, s32[2048,32]{0,1:T(8,128)S(1)} %dynamic-slice_bitcast_fusion.2), kind=kOutput, calls=%fused_computation.6.clone.2 | convolution fusion | flops 553648128 | bytes 852480 | tf_op jit(solution)/shard_map/while/body/eval_jaxpr/rfb,rs->fsb/dot_general | solution.py:61
  263.5 1.0 dynamic-slice_bitcast_fusion.2
  264.6 16.8 %fusion.19 = f32[16,32,16,256]{3,2,1,0:T(8,128)} fusion(f32[16,32,16,256]{3,2,1,0:T(8,128)} %get-tuple-element.97, s32[]{:T(128)} %get-tuple-element.96, bf16[2048,16,1]{0,1,2:T(8,128)(2,1)S(1)} %reshape.85, s32[2048,32]{0,1:T(8,128)S(1)} %dynamic-slice_bitcast_fusion.2), kind=kOutput, calls=%fused_computation.6.clone.2 | convolution fusion | flops 553648128 | bytes 852480 | tf_op jit(solution)/shard_map/while/body/eval_jaxpr/rfb,rs->fsb/dot_general | solution.py:61
  281.4 1.0 dynamic-slice_bitcast_fusion.2
  282.4 0.1 multiply_convert_fusion.2
  282.5 16.8 %fusion.19 = f32[16,32,16,256]{3,2,1,0:T(8,128)} fusion(f32[16,32,16,256]{3,2,1,0:T(8,128)} %get-tuple-element.97, s32[]{:T(128)} %get-tuple-element.96, bf16[2048,16,1]{0,1,2:T(8,128)(2,1)S(1)} %reshape.85, s32[2048,32]{0,1:T(8,128)S(1)} %dynamic-slice_bitcast_fusion.2), kind=kOutput, calls=%fused_computation.6.clone.2 | convolution fusion | flops 553648128 | bytes 852480 | tf_op jit(solution)/shard_map/while/body/eval_jaxpr/rfb,rs->fsb/dot_general | solution.py:61
  299.4 74.4 %reduce-scatter.2.cloned.1.call-done = f32[64,16,256]{2,1,0:T(8,128)} async-done(((f32[512,16,256]{2,1,0:T(8,128)}), f32[64,16,256]{2,1,0:T(8,128)}) %reduce-scatter.2.cloned.1.call-update) | async-done | bytes 1048592 | tf_op jit(solution)/shard_map/reduce_scatter | solution.py:69
  373.7 1.5 collective-permute-start
  375.2 23.4 %collective-permute-done = f32[64,16,256]{2,1,0:T(8,128)S(1)} collective-permute-done((f32[64,16,256]{2,1,0:T(8,128)}, f32[64,16,256]{2,1,0:T(8,128)S(1)}, u32[]{:S(2)}, u32[]{:S(2)}) %collective-permute-start) | collective-permute-done | bytes 1048608 | tf_op jit(solution)/shard_map/ppermute | solution.py:74
  398.7 1.4 add.11
  400.1 2.5 collective-permute-start.1
  402.6 44.8 %collective-permute-done.1 = f32[64,16,256]{2,1,0:T(8,128)S(1)} collective-permute-done((f32[64,16,256]{2,1,0:T(8,128)S(1)}, f32[64,16,256]{2,1,0:T(8,128)S(1)}, u32[]{:S(2)}, u32[]{:S(2)}) %collective-permute-start.1) | collective-permute-done | bytes 1048608 | tf_op jit(solution)/shard_map/ppermute | solution.py:74
  447.4 0.7 fusion.8
  448.1 0.6 reshape.80
  448.7 1.4 fusion.13
  450.1 0.1 copy.29
  450.2 0.1 copy.23
  450.3 1.5 reduce_sum.27
  451.8 3.1 copy.28
  455.0 0.4 broadcast_divide_fusion
  455.3 2.0 multiply_reduce_fusion
  457.3 0.3 reduce_max.18
  457.6 0.1 copy.26
  457.7 0.1 bitcast_reduce_fusion
  457.8 12.5 %pmax.7 = f32[2,4]{1,0:T(2,128)} all-reduce(f32[2,4]{1,0:T(2,128)S(1)} %bitcast_reduce_fusion), channel_id=1, replica_groups=mesh['rows'=4,'feat'=8] {'feat'}, use_global_device_ids=true, to_apply=%region_8.9 | all-reduce | flops 8 | bytes 64 | tf_op jit(solution)/shard_map/pmax | solution.py:76
  (36 shorter events, 0.9 us)
Async XLA Ops:
  7.2 5.5 %copy-start.1 = (s32[2,2048]{1,0:T(2,128)S(1)}, s32[2,2048]{1,0:T(2,128)}, u32[]{:S(2)}) copy-start(s32[2,2048]{1,0:T(2,128)} %param.8) | copy-start | bytes 49156
  7.2 5.5 %copy-start.3 = (s32[2048]{0:T(1024)S(1)}, s32[2048]{0:T(1024)}, u32[]{:S(2)}) copy-start(s32[2048]{0:T(1024)} %param.9) | copy-start | bytes 24580
  7.2 5.5 %copy-start.2 = (s32[2,2048]{1,0:T(2,128)S(1)}, s32[2,2048]{1,0:T(2,128)}, u32[]{:S(2)}) copy-start(s32[2,2048]{1,0:T(2,128)} %param.7) | copy-start | bytes 49156
  7.2 366.5 %reduce-scatter.2.cloned.1.call-start = ((), (), s32[]{:S(2)}) async-start(), calls=%async_computation.1 | async-start | bytes 9437184 | tf_op jit(solution)/shard_map/reduce_scatter | solution.py:69
  373.7 24.9 %collective-permute-start = (f32[64,16,256]{2,1,0:T(8,128)}, f32[64,16,256]{2,1,0:T(8,128)S(1)}, u32[]{:S(2)}, u32[]{:S(2)}) collective-permute-start(f32[64,16,256]{2,1,0:T(8,128)} %reduce-scatter.2.cloned.1.call-done), channel_id=1, source_target_pairs={{0,8},{8,0},{16,24},{24,16},{1,9},{9,1},{17,25},{25,17},{2,10},{10... | collective-permute-start | bytes 3145736 | tf_op jit(solution)/shard_map/ppermute | solution.py:74
  400.1 47.3 %collective-permute-start.1 = (f32[64,16,256]{2,1,0:T(8,128)S(1)}, f32[64,16,256]{2,1,0:T(8,128)S(1)}, u32[]{:S(2)}, u32[]{:S(2)}) collective-permute-start(f32[64,16,256]{2,1,0:T(8,128)S(1)} %add.11), channel_id=1, source_target_pairs={{0,16},{8,24},{16,0},{24,8},{1,17},{9,25},{17,1},{25,9},{2,18},{10... | collective-permute-start | bytes 3145736 | tf_op jit(solution)/shard_map/ppermute | solution.py:74
  457.7 12.6 %copy-start = (f32[64,2,4]{0,2,1:T(4,128)}, f32[64,2,4]{0,2,1:T(4,128)S(1)}, u32[]{:S(2)}) copy-start(f32[64,2,4]{0,2,1:T(4,128)S(1)} %copy.26) | copy-start | bytes 6148
Sparse Core Ops, SparseCore 0:
  299.5 74.2 reduce-scatter.1
